TPU v7x, 32 devices: a whole 2x2x4 slice. The times are simulated.
32 devices in a mesh: dp: 8 (over z, y), tp: 4 (over x, core).
Axes of the slice: x: 2, y: 2, z: 4, core: 2. Of those that a mesh axis runs over, the one named last changes fastest.
Arguments:
- tokens: bfloat16 [768, 2880], P('dp', 'tp'), may hold values from -100 to 100
- attn_gain: float32 [2880], replicated, may hold values from 0.1 to 1.9
- w_query: bfloat16 [2880, 2048], P(None, 'tp'), may hold values from -0.109375 to 0.109375
- w_keyvalue: bfloat16 [2880, 8, 128], P(None, 'tp'), may hold values from -0.109375 to 0.109375
- attn_sinks: float32 [32], P('tp'), may hold values from 2 to 6
- w_out: bfloat16 [2048, 2880], P('tp'), may hold values from -0.125 to 0.125
- window_cache: bfloat16 [768, 8, 128, 128], P('dp', 'tp'), may hold values from -1000 to 1000
- positions: int32 [768], P('dp'), may hold values from 0 to 511
- moe_gain: float32 [2880], replicated, may hold values from 0.1 to 1.9
- router: bfloat16 [2880, 8], P('tp'), may hold values from -0.109375 to 0.109375
- gate_up: bfloat16 [8, 2880, 2, 2880], P('dp', None, None, 'tp'), may hold values from -0.109375 to 0.109375
- w_down: bfloat16 [8, 2880, 2880], P('dp', None, 'tp'), may hold values from -0.109375 to 0.109375
- expert_ids: int32 [768, 4], P('dp'), may hold values from 0 to 7, all different within a row; in each aligned block of 96 rows (0 to 95, 96 to 191, ...) at most 96 rows name the same one
Outputs:
- layer_out: float32 [768, 2880], P('dp', 'tp')
Inputs may be any that keep to these rules, and one draw needn't show every extreme that they name: `expert_ids`: each row names 4 different experts. Within the rows of one index of dp no expert is named by more than 96 rows, a bound that some of these blocks reach.
All inputs are finite; a program needn't handle non-finite values.
Results may differ from a plain program's by a relative error of at most 0.0066.
Values may be sent and summed in bfloat16 or wider, within the bound.
A program may use at most 128 MiB of HBM per device.

v0:
```python
import jax
import jax.numpy as jnp
from jax import lax
from jax.sharding import PartitionSpec as P

norm_eps = 1e-05
rope_base = 150000.0
glu_alpha = 1.702


def rope_tables(positions, head_size):
    half_size = head_size // 2
    exponent = jnp.arange(half_size, dtype=jnp.float32) * (2.0 / head_size)
    inverse = jnp.power(jnp.float32(rope_base), -exponent)
    angles = positions.astype(jnp.float32)[:, None] * inverse[None, :]
    return (jnp.cos(angles), jnp.sin(angles))


def rotate(values, cosine, sine_table):
    half_size = values.shape[-1] // 2
    first_half = values[..., :half_size]
    second_half = values[..., half_size:]
    return jnp.concatenate(
        [
            first_half * cosine - second_half * sine_table,
            second_half * cosine + first_half * sine_table,
        ],
        axis=-1,
    )


def on_device(
    tokens,
    attn_gain,
    w_query,
    w_keyvalue,
    attn_sinks,
    w_out,
    window_cache,
    positions,
    moe_gain,
    router,
    gate_up,
    w_down,
    expert_ids,
):
    tp_count = lax.axis_size("tp")
    dp_count = lax.axis_size("dp")
    seq_count, col_count = tokens.shape
    full_width = col_count * tp_count
    col_start = lax.axis_index("tp") * col_count
    head_size = w_keyvalue.shape[2] // 2
    kv_local = w_keyvalue.shape[1]
    q_local = w_query.shape[1] // head_size
    group_size = q_local // kv_local
    window = window_cache.shape[2]
    attn_slice = lax.dynamic_slice_in_dim(attn_gain, col_start, col_count)
    moe_slice = lax.dynamic_slice_in_dim(moe_gain, col_start, col_count)
    tok_wide = tokens.astype(jnp.float32)
    attn_sq = lax.psum(jnp.sum(tok_wide * tok_wide, axis=1), "tp")
    normed = (
        tok_wide * lax.rsqrt(attn_sq / full_width + norm_eps)[:, None] * attn_slice[None, :]
    ).astype(jnp.bfloat16)
    kv_flat = w_keyvalue.reshape(full_width, kv_local * 2 * head_size)
    piece_rows = lax.all_gather(normed, "tp", axis=1, tiled=True)
    queries = jnp.dot(piece_rows, w_query, preferred_element_type=jnp.float32)
    fresh_rows = jnp.dot(piece_rows, kv_flat, preferred_element_type=jnp.float32)
    cosine, sine_table = rope_tables(positions, head_size)
    rot_queries = rotate(
        queries.reshape(seq_count, q_local, head_size), cosine[:, None, :], sine_table[:, None, :]
    ).astype(jnp.bfloat16)
    fresh_rows = fresh_rows.reshape(seq_count, kv_local, 2 * head_size)
    new_key = rotate(fresh_rows[..., :head_size], cosine[:, None, :], sine_table[:, None, :])
    new_entry = jnp.concatenate([new_key, fresh_rows[..., head_size:]], axis=-1).astype(
        jnp.bfloat16
    )
    slot_ids = jnp.arange(window, dtype=jnp.int32)
    is_current = slot_ids[None, :] == (positions % window)[:, None]
    cache_now = jnp.where(is_current[:, None, :, None], new_entry[:, :, None, :], window_cache)
    is_valid = (positions[:, None] - slot_ids[None, :]) % window <= positions[:, None]
    grouped = rot_queries.reshape(seq_count, kv_local, group_size, head_size)
    scores = jnp.einsum(
        "skgh,skwh->skgw", grouped, cache_now[..., :head_size], preferred_element_type=jnp.float32
    ) * head_size ** (-0.5)
    scores = jnp.where(is_valid[:, None, None, :], scores, -jnp.inf)
    sink_col = attn_sinks.reshape(kv_local, group_size)[None, :, :, None]
    peak_score = jnp.maximum(jnp.max(scores, axis=-1, keepdims=True), sink_col)
    raised = jnp.exp(scores - peak_score)
    denominator = jnp.sum(raised, axis=-1, keepdims=True) + jnp.exp(sink_col - peak_score)
    prob_bf = (raised / denominator).astype(jnp.bfloat16)
    attended = jnp.einsum(
        "skgw,skwh->skgh", prob_bf, cache_now[..., head_size:], preferred_element_type=jnp.float32
    ).astype(jnp.bfloat16)
    partial_out = jnp.dot(
        attended.reshape(seq_count, q_local * head_size), w_out, preferred_element_type=jnp.float32
    )
    residual = tok_wide + lax.psum_scatter(
        partial_out.astype(jnp.bfloat16), "tp", scatter_dimension=1, tiled=True
    ).astype(jnp.float32)
    experts = router.shape[1]
    top_count = expert_ids.shape[1]
    local_experts = gate_up.shape[0]
    ff_local = gate_up.shape[3]
    capacity = min(seq_count, max(2, 8 * seq_count * top_count // (3 * experts)))
    moe_sq = jnp.sum(residual * residual, axis=1)
    router_wide = router.astype(jnp.float32)
    total_sq = lax.psum(moe_sq, "tp")
    moe_scale = lax.rsqrt(total_sq / full_width + norm_eps)[:, None]
    scaled = residual * moe_scale * moe_slice[None, :]
    logits = lax.psum(jnp.dot(scaled, router_wide, precision=lax.Precision.HIGHEST), "tp")
    hidden_rows = scaled.astype(jnp.bfloat16)
    expert_iota = jnp.arange(experts, dtype=jnp.int32)
    chosen = expert_ids[:, :, None] == expert_iota[None, None, :]
    picked = jnp.sum(jnp.where(chosen, logits[:, None, :], 0.0), axis=-1)
    raised_logits = jnp.exp(picked)
    route_weights = raised_logits / jnp.sum(raised_logits, axis=1, keepdims=True)
    assign = expert_ids.reshape(-1)
    onehot = (assign[:, None] == expert_iota[None, :]).astype(jnp.int32)
    earlier = jnp.cumsum(onehot, axis=0) - onehot
    slot_of = jnp.sum(earlier * onehot, axis=1)
    target = (assign * capacity + slot_of).reshape(seq_count, top_count)
    spot_ids = jnp.arange(experts * capacity, dtype=jnp.int32)
    slot_hits = target[:, :, None] == spot_ids[None, None, :]
    placer = jnp.transpose(jnp.any(slot_hits, axis=1)).astype(jnp.bfloat16)
    combiner = jnp.sum(jnp.where(slot_hits, route_weights[:, :, None], 0.0), axis=1)
    gate_up_flat = gate_up.reshape(local_experts, full_width, 2 * ff_local)
    placed = jnp.dot(placer, hidden_rows, preferred_element_type=jnp.float32).astype(jnp.bfloat16)
    mixed_in = jnp.einsum(
        "gecd,edf->gecf",
        lax.all_gather(
            lax.all_to_all(
                placed.reshape(dp_count, local_experts, capacity, hidden_rows.shape[1]),
                "dp",
                split_axis=0,
                concat_axis=0,
                tiled=True,
            ),
            "tp",
            axis=3,
            tiled=True,
        ),
        gate_up_flat,
        preferred_element_type=jnp.float32,
    )
    gate_part = mixed_in[..., :ff_local]
    up_part = mixed_in[..., ff_local:]
    act_rows = (gate_part * jax.nn.sigmoid(glu_alpha * gate_part) * (up_part + 1.0)).astype(
        jnp.bfloat16
    )
    answered = jnp.einsum(
        "gecf,efd->gecd",
        lax.all_gather(act_rows, "tp", axis=3, tiled=True),
        w_down,
        preferred_element_type=jnp.float32,
    ).astype(jnp.bfloat16)
    returned = lax.all_to_all(answered, "dp", split_axis=0, concat_axis=0, tiled=True)
    flat_back = returned.reshape(experts * capacity, col_count).astype(jnp.float32)
    moe_out = jnp.dot(combiner, flat_back, precision=lax.Precision.HIGHEST)
    return residual + moe_out


def solution(mesh):
    in_specs = (
        P("dp", "tp"),
        P(),
        P(None, "tp"),
        P(None, "tp", None),
        P("tp"),
        P("tp", None),
        P("dp", "tp", None, None),
        P("dp"),
        P(),
        P("tp", None),
        P("dp", None, None, "tp"),
        P("dp", None, "tp"),
        P("dp", None),
    )
    out_specs = P("dp", "tp")
    return jax.shard_map(
        on_device, mesh=mesh, in_specs=in_specs, out_specs=out_specs, check_vma=False
    )
```

profile of v0, /device:TPU:0, one launch (start us, length us, event | category | flops | bytes accessed | tf_op | source)
XLA Modules:
  0.0 306.0 jit_solution(1373459359515891442)
XLA Ops:
  7.8 8.4 %psum.21 = f32[96]{0:T(128)S(1)} all-reduce(f32[96]{0:T(128)S(1)} %fusion.37), channel_id=1, replica_groups=mesh['dp'=8,'tp'=4] {'tp'}, use_global_device_ids=true, to_apply=%region_1.0 | all-reduce | flops 96 | bytes 768 | tf_op jit(solution)/shard_map/psum | solution.py:60
  17.9 6.7 %all-gather = bf16[4,720,96]{1,2,0:T(8,128)(2,1)S(1)} all-gather(bf16[1,720,96]{1,2,0:T(8,128)(2,1)S(1)} %fusion.48), channel_id=1, replica_groups=mesh['dp'=8,'tp'=4] {'tp'}, dimensions={0}, use_global_device_ids=true | all-gather | bytes 691200 | tf_op jit(solution)/shard_map/all_gather | solution.py:65
  28.9 4.9 %copy.111 = bf16[2880,2,128]{0,2,1:T(8,128)(2,1)} copy(bf16[2880,2,128]{2,1,0:T(2,128)(2,1)} %param.16) | data formatting | bytes 2949120 | tf_op jit(solution)/shard_map/dot_general | solution.py:67
  35.3 2.0 fusion.19
  40.4 8.7 %copy.95 = bf16[96,2,128,128]{2,3,1,0:T(8,128)(2,1)} copy(bf16[96,2,128,128]{3,2,1,0:T(8,128)(2,1)} %param.19) | data formatting | bytes 12582912 | tf_op args[6]
  49.1 3.1 %fusion.65 = f32[96,512]{0,1:T(8,128)S(1)} fusion(bf16[2880,96]{0,1:T(8,128)(2,1)S(1)} %copy-done.3, bf16[2880,512]{1,0:T(8,128)(2,1)} %param.15), kind=kOutput, calls=%fused_computation.91 | convolution fusion | flops 283115520 | bytes 3698688 | tf_op jit(solution)/shard_map/dot_general | solution.py:66
  52.7 7.2 %broadcast_select_fusion = bf16[96,2,128,128]{2,3,1,0:T(8,128)(2,1)S(1)} fusion(bf16[96,2,128,128]{2,3,1,0:T(8,128)(2,1)} %copy.95, pred[96,128]{1,0:T(8,128)(4,1)} %iota_compare_fusion.1, bf16[96,2,128]{2,1,0:T(2,128)(2,1)} %copy.94), kind=kLoop, calls=%fused_computation | loop fusion | flops 3145728 | bytes 12644352 | tf_op jit(solution)/shard_map/jit(_where)/select_n | solution.py:79
  63.8 1.9 convolution_convert_fusion
  65.7 2.2 copy.112
  70.7 21.4 %reduce-scatter.4.cloned.1.call-done = bf16[720,96]{1,0:T(8,128)(2,1)} async-done(((bf16[2880,96]{1,0:T(8,128)(2,1)}), bf16[720,96]{1,0:T(8,128)(2,1)}) %reduce-scatter.4.cloned.1.call-update) | async-done | bytes 138256
  93.3 5.8 %psum.22 = f32[96]{0:T(128)S(1)} all-reduce(f32[96]{0:T(128)S(1)} %multiply_reduce_fusion), channel_id=1, replica_groups=mesh['dp'=8,'tp'=4] {'tp'}, use_global_device_ids=true, to_apply=%region_9.10 | all-reduce | flops 96 | bytes 768 | tf_op jit(solution)/shard_map/psum | solution.py:107
  100.3 34.2 %all_to_all.10 = bf16[8,1,96,720]{3,2,1,0:T(8,128)(2,1)S(1)} all-to-all(bf16[8,1,96,720]{3,2,1,0:T(8,128)(2,1)S(1)} %bitcast.88), channel_id=1, replica_groups=mesh['dp'=8,'tp'=4] {'dp'}, dimensions={0} | all-to-all | bytes 2211840 | tf_op jit(solution)/shard_map/all_to_all | solution.py:131
  134.5 1.9 copy.102
  136.7 41.8 %all-gather.4.cloned.1.call-done = bf16[8,1,96,2880]{2,0,1,3:T(8,128)(2,1)} async-done(((bf16[8,1,96,720]{2,0,1,3:T(8,128)(2,1)}), bf16[8,1,96,2880]{2,0,1,3:T(8,128)(2,1)}) %all-gather.4.cloned.1.call-update) | async-done | bytes 4423696 | tf_op jit(solution)/shard_map/all_gather | solution.py:130
  178.5 8.3 %copy.103 = bf16[8,1,96,2880]{3,2,0,1:T(8,128)(2,1)} copy(bf16[8,1,96,2880]{2,0,1,3:T(8,128)(2,1)} %all-gather.4.cloned.1.call-done) | data formatting | bytes 8847360 | tf_op jit(solution)/shard_map/all_gather | solution.py:130
  186.8 11.4 %fusion.5 = f32[8,1,96,1440]{3,2,0,1:T(8,128)S(1)} fusion(bf16[2880,1440,1]{0,1,2:T(8,128)(2,1)} %bitcast.104, bf16[8,1,96,2880]{3,2,0,1:T(8,128)(2,1)} %copy.103), kind=kOutput, calls=%fused_computation.6 | convolution fusion | flops 6370099200 | bytes 17141760 | tf_op jit(solution)/shard_map/gecd,edf->gecf/dot_general | solution.py:128
  199.1 1.9 copy.104
  201.0 44.3 %all-gather.6.cloned.1.call-done = bf16[8,1,96,2880]{2,0,1,3:T(8,128)(2,1)} async-done(((bf16[8,1,96,720]{2,0,1,3:T(8,128)(2,1)}), bf16[8,1,96,2880]{2,0,1,3:T(8,128)(2,1)}) %all-gather.6.cloned.1.call-update) | async-done | bytes 4423696 | tf_op jit(solution)/shard_map/all_gather | solution.py:152
  245.3 8.3 %copy.105 = bf16[8,1,96,2880]{3,2,0,1:T(8,128)(2,1)} copy(bf16[8,1,96,2880]{2,0,1,3:T(8,128)(2,1)} %all-gather.6.cloned.1.call-done) | data formatting | bytes 8847360 | tf_op jit(solution)/shard_map/all_gather | solution.py:152
  253.6 8.6 %fusion.21 = bf16[8,1,96,720]{3,2,1,0:T(8,128)(2,1)} fusion(bf16[1,2880,720]{1,2,0:T(8,128)(2,1)} %param.24, bf16[8,1,96,2880]{3,2,0,1:T(8,128)(2,1)} %copy.105), kind=kOutput, calls=%fused_computation.19 | convolution fusion | flops 3185602560 | bytes 9676800 | tf_op jit(solution)/shard_map/gecf,efd->gecd/dot_general | solution.py:150
  262.2 5.5 %all-to-all-start.1 = ((bf16[8,1,96,720]{3,2,1,0:T(8,128)(2,1)}), bf16[8,1,96,720]{3,2,1,0:T(8,128)(2,1)}, u32[]{:S(2)}, u32[]{:S(2)}) async-start(bf16[8,1,96,720]{3,2,1,0:T(8,128)(2,1)} %fusion.21), calls=%async_computation.1 | async-start | bytes 2359296 | tf_op jit(solution)/shard_map/all_to_all | solution.py:156
  268.0 6.2 %psum.23 = f32[96,8]{0,1:T(8,128)S(1)} all-reduce(f32[96,8]{0,1:T(8,128)S(1)} %fusion.41), channel_id=1, replica_groups=mesh['dp'=8,'tp'=4] {'tp'}, use_global_device_ids=true, to_apply=%region_10.11 | all-reduce | flops 768 | bytes 6144 | tf_op jit(solution)/shard_map/psum | solution.py:110
  274.5 22.3 %all-to-all-done.1 = bf16[8,1,96,720]{3,2,1,0:T(8,128)(2,1)} async-done(((bf16[8,1,96,720]{3,2,1,0:T(8,128)(2,1)}), bf16[8,1,96,720]{3,2,1,0:T(8,128)(2,1)}, u32[]{:S(2)}, u32[]{:S(2)}) %all-to-all-start.1) | async-done | bytes 1105952 | tf_op jit(solution)/shard_map/all_to_all | solution.py:156
  296.8 2.7 convolution_add_fusion
  (80 shorter events, 23.0 us)
Async XLA Ops:
  6.5 57.3 %copy-start = (bf16[512,2880]{0,1:T(8,128)(2,1)S(1)}, bf16[512,2880]{0,1:T(8,128)(2,1)}, u32[]{:S(2)}) copy-start(bf16[512,2880]{0,1:T(8,128)(2,1)} %param.18) | copy-start | bytes 8847364
  6.5 21.1 %copy-start.7 = (s32[96]{0:T(128)S(1)}, s32[96]{0:T(128)}, u32[]{:S(2)}) copy-start(s32[96]{0:T(128)} %param.20) | copy-start | bytes 1156
  6.5 85.6 %reduce-scatter.4.cloned.1.call-start = ((), (), s32[]{:S(2)}) async-start(), calls=%async_computation.5 | async-start | bytes 921600
  27.6 7.7 %copy-start.4 = (bf16[2880,96,1]{0,1,2:T(8,128)(2,1)S(1)}, bf16[2880,96,1]{0,1,2:T(8,128)(2,1)}, u32[]{:S(2)}) copy-start(bf16[2880,96,1]{0,1,2:T(8,128)(2,1)} %reshape.248) | copy-start | bytes 1658884
  40.4 8.7 %copy-start.3 = (bf16[2880,96]{0,1:T(8,128)(2,1)S(1)}, bf16[2880,96]{0,1:T(8,128)(2,1)}, u32[]{:S(2)}) copy-start(bf16[2880,96]{0,1:T(8,128)(2,1)} %reshape.247) | copy-start | bytes 1658884
  49.1 3.5 %copy-start.9 = (f32[8]{0:T(128)S(1)}, f32[8]{0:T(128)}, u32[]{:S(2)}) copy-start(f32[8]{0:T(128)} %param.17) | copy-start | bytes 100
  52.7 7.2 %copy-start.6 = (pred[96,128]{1,0:T(8,128)(4,1)S(1)}, pred[96,128]{1,0:T(8,128)(4,1)}, u32[]{:S(2)}) copy-start(pred[96,128]{1,0:T(8,128)(4,1)} %fusion.54) | copy-start | bytes 36868
  63.6 4.4 %copy-start.5 = (s32[96,4]{0,1:T(4,128)S(1)}, s32[96,4]{0,1:T(4,128)}, u32[]{:S(2)}) copy-start(s32[96,4]{0,1:T(4,128)} %param.25) | copy-start | bytes 4612
  63.8 29.4 %copy-start.2 = (bf16[96,720]{1,0:T(8,128)(2,1)S(1)}, bf16[96,720]{1,0:T(8,128)(2,1)}, u32[]{:S(2)}) copy-start(bf16[96,720]{1,0:T(8,128)(2,1)} %param.13) | copy-start | bytes 414724
  67.9 110.5 %all-gather.4.cloned.1.call-start = ((), (), s32[]{:S(2)}) async-start(), calls=%async_computation.3 | async-start | bytes 7372800 | tf_op jit(solution)/shard_map/all_gather | solution.py:130
  136.5 108.8 %all-gather.6.cloned.1.call-start = ((), (), s32[]{:S(2)}) async-start(), calls=%async_computation.4 | async-start | bytes 7372800 | tf_op jit(solution)/shard_map/all_gather | solution.py:152
  253.6 14.1 %copy-start.8 = (bf16[720,8]{0,1:T(8,128)(2,1)S(1)}, bf16[720,8]{0,1:T(8,128)(2,1)}, u32[]{:S(2)}) copy-start(bf16[720,8]{0,1:T(8,128)(2,1)} %param.22) | copy-start | bytes 34564
  253.6 45.9 %copy-start.1 = (bf16[512,2880]{0,1:T(8,128)(2,1)S(1)}, bf16[512,2880]{0,1:T(8,128)(2,1)}, u32[]{:S(2)}) copy-start(bf16[512,2880]{0,1:T(8,128)(2,1)} %param.18) | copy-start | bytes 8847364
  262.2 34.6 %all-to-all-start.1 = ((bf16[8,1,96,720]{3,2,1,0:T(8,128)(2,1)}), bf16[8,1,96,720]{3,2,1,0:T(8,128)(2,1)}, u32[]{:S(2)}, u32[]{:S(2)}) async-start(bf16[8,1,96,720]{3,2,1,0:T(8,128)(2,1)} %fusion.21), calls=%async_computation.1 | async-start | bytes 2359296 | tf_op jit(solution)/shard_map/all_to_all | solution.py:156
Sparse Core Ops, SparseCore 0:
  68.0 24.0 reduce-scatter.3
  136.6 41.8 all-gather.3
  201.1 44.1 all-gather.5
where the time goes:
time: 307 us; the launch traced here: 306 us
  waiting for transfers between devices  130 us (42%)
  blocking collectives  61.2 us (20%)
  local copies, waits for them, and re-layouts  46.1 us (15%)
  matrix products  33.5 us (11%)
  other arithmetic  16.2 us (5%)
  between operations  13.4 us (4%)
  starting transfers between devices  5.78 us (2%)
    all_gather x1, waiting for transfers between devices, on_device(): lax.all_gather(act_rows, 'tp', axis=3, tiled=True)  44.3 us
    all_gather x1, waiting for transfers between devices, on_device(): lax.all_gather(lax.all_to_all(placed.reshape(dp_count, local_experts, cap...  41.8 us
    all_to_all x1, blocking collectives, on_device(): lax.all_to_all(placed.reshape(dp_count, local_experts, capacity, hidden_r...  34.2 us
    all_to_all x1, waiting for transfers between devices, on_device(): lax.all_to_all(answered, 'dp', split_axis=0, concat_axis=0, tiled=True)  22.3 us
    unnamed x4, waiting for transfers between devices  21.5 us
    unnamed x28, local copies, waits for them, and re-layouts  14.7 us
    dot_general x1, matrix products, on_device(): jnp.einsum('gecd,edf->gecf', lax.all_gather(lax.all_to_all(placed.reshape...  11.4 us
    dot_general x1, matrix products, on_device(): jnp.einsum('gecf,efd->gecd', lax.all_gather(act_rows, 'tp', axis=3, tiled...  8.57 us
  transfers between devices with their start and end apart: 4, of which 4 were waited for; matrix products, arithmetic and copies ran while one was open for 1% of the time, Pallas kernels for 0%

commit v1 on v0

--- a/solution.py
+++ b/solution.py
@@ -1,6 +1,11 @@
+import functools
+import math
+
 import jax
 import jax.numpy as jnp
 from jax import lax
+from jax.experimental import pallas as pl
+from jax.experimental.pallas import tpu as pltpu
 from jax.sharding import PartitionSpec as P
 
 norm_eps = 1e-05
@@ -26,6 +31,278 @@
             second_half * cosine + first_half * sine_table,
         ],
         axis=-1,
+    )
+
+
+MESH = pl.DeviceIdType.MESH
+CORES = 2
+
+
+def greet(partners):
+    barrier = pltpu.get_barrier_semaphore()
+    for partner in partners:
+        pl.semaphore_signal(barrier, inc=1, device_id=partner, device_id_type=MESH)
+    pl.semaphore_wait(barrier, len(partners))
+
+
+def feature_gather_kernel(tp, chunks, x_ref, out_ref, buf, own_sem, send_x, send_c, recv):
+    chips = tp // CORES
+    dp_id = lax.axis_index("dp")
+    me = lax.axis_index("tp")
+    core = lax.rem(me, CORES)
+    chip = me // CORES
+    rows, cols = x_ref.shape
+    step = rows // chunks
+    twin = (dp_id, chip * CORES + (1 - core))
+    others = [lax.rem(chip + d, chips) * CORES + core for d in range(1, chips)]
+    sources = [lax.rem(chip + chips - d, chips) * CORES + core for d in range(1, chips)]
+    own = pltpu.make_async_copy(x_ref, buf.at[me], own_sem)
+    own.start()
+    greet([twin] + [(dp_id, other) for other in others])
+
+    def piece(k):
+        return pl.ds(k * step, step)
+
+    def send(src, origin, k, sem, target):
+        return pltpu.make_async_remote_copy(
+            src_ref=src, dst_ref=buf.at[origin, piece(k)], send_sem=sem,
+            recv_sem=recv.at[origin, k], device_id=target, device_id_type=MESH)
+
+    sent = []
+    for k in range(chunks):
+        for d in range(chips - 1):
+            sent.append(send(x_ref.at[piece(k)], me, k, send_x.at[d, k], (dp_id, others[d])))
+            sent[-1].start()
+    for k in range(chunks):
+        sent.append(send(x_ref.at[piece(k)], me, k, send_c.at[0, k], twin))
+        sent[-1].start()
+    own.wait()
+    for k in range(chunks):
+        for d in range(chips - 1):
+            origin = sources[d]
+            forward = send(buf.at[origin, piece(k)], origin, k, send_c.at[d + 1, k], twin)
+            forward.wait_recv()
+            forward.start()
+            sent.append(forward)
+        if k:
+            finish(tp, k - 1, step, chip, core, chips, buf, recv, out_ref, send, twin)
+    finish(tp, chunks - 1, step, chip, core, chips, buf, recv, out_ref, send, twin)
+    for copy in sent:
+        copy.wait_send()
+
+
+def finish(tp, k, step, chip, core, chips, buf, recv, out_ref, send, twin):
+    cols = buf.shape[2]
+    part = pl.ds(k * step, step)
+    for d in range(chips):
+        origin = lax.rem(chip + d, chips) * CORES + (1 - core)
+        pltpu.make_async_remote_copy(
+            src_ref=buf.at[origin, part], dst_ref=buf.at[origin, part], send_sem=recv.at[origin, k],
+            recv_sem=recv.at[origin, k], device_id=twin, device_id_type=MESH).wait_recv()
+    for t in range(tp):
+        out_ref[part, t * cols:(t + 1) * cols] = buf[t, part, :]
+
+
+def feature_gather(x, tp, chunks, collective_id):
+    rows, cols = x.shape
+    chips = tp // CORES
+    return pl.pallas_call(
+        functools.partial(feature_gather_kernel, tp, chunks),
+        out_shape=jax.ShapeDtypeStruct((rows, tp * cols), x.dtype),
+        in_specs=[pl.BlockSpec(memory_space=pltpu.VMEM)],
+        out_specs=pl.BlockSpec(memory_space=pltpu.VMEM),
+        scratch_shapes=[
+            pltpu.VMEM((tp, rows, cols), x.dtype),
+            pltpu.SemaphoreType.DMA,
+            pltpu.SemaphoreType.DMA((max(chips - 1, 1), chunks)),
+            pltpu.SemaphoreType.DMA((chips, chunks)),
+            pltpu.SemaphoreType.DMA((tp, chunks)),
+        ],
+        compiler_params=pltpu.CompilerParams(
+            collective_id=collective_id, has_side_effects=True, vmem_limit_bytes=48 * 2**20),
+        cost_estimate=pl.CostEstimate(flops=0, bytes_accessed=rows * cols * tp * 16, transcendentals=0),
+    )(x)
+
+
+def full_gather_kernel(dp, ny, tp, x_ref, out_ref, buf, own_sem, send_z, send_x, send_y, send_c, recv):
+    nz, nx = dp // ny, tp // CORES
+    dp_id = lax.axis_index("dp")
+    me = lax.axis_index("tp")
+    core, x = lax.rem(me, CORES), me // CORES
+    z, y = dp_id // ny, lax.rem(dp_id, ny)
+    rows, cols = x_ref.shape
+    half = rows // 2
+
+    def place(pz, py, px, pc=core):
+        return (pz * ny + py, px * CORES + pc)
+
+    def around(v, d, n):
+        return lax.rem(v + d, n)
+
+    own = pltpu.make_async_copy(x_ref, buf.at[dp_id, me], own_sem)
+    own.start()
+    twin = place(z, y, x, 1 - core)
+    x_others = [place(z, y, around(x, d, nx)) for d in range(1, nx)]
+    y_others = [place(z, around(y, d, ny), x) for d in range(1, ny)]
+    ring = [place(lax.rem(z + d, nz), y, x) for d in sorted({1 % nz, nz - 1} - {0})]
+    greet([twin] + x_others + y_others + ring)
+    own.wait()
+
+    def copy(origin, h, sem, target):
+        view = buf.at[origin[0], origin[1], pl.ds(h * half, half)]
+        return pltpu.make_async_remote_copy(
+            src_ref=view, dst_ref=view, send_sem=sem.at[origin[0], origin[1] // CORES, h],
+            recv_sem=recv.at[origin[0], origin[1], h], device_id=target, device_id_type=MESH)
+
+    def arrived(origin, h):
+        view = buf.at[origin[0], origin[1], pl.ds(h * half, half)]
+        pltpu.make_async_remote_copy(
+            src_ref=view, dst_ref=view, send_sem=recv.at[origin[0], origin[1], h],
+            recv_sem=recv.at[origin[0], origin[1], h], device_id=twin, device_id_type=MESH).wait_recv()
+
+    def to_x(origin, h, act):
+        for d in range(nx - 1):
+            act(copy(origin, h, send_x.at[d], x_others[d]))
+
+    def to_y(origin, h, act):
+        for d in range(ny - 1):
+            act(copy(origin, h, send_y.at[d], y_others[d]))
+
+    def to_twin(origin, h, act):
+        act(copy(origin, h, send_c, twin))
+
+    def start(c):
+        c.start()
+
+    def ended(c):
+        c.wait_send()
+
+    def spread(origin, act):
+        to_x(origin, 0, act)
+        to_y(origin, 1, act)
+        to_y(origin, 0, act)
+        to_x(origin, 1, act)
+        for h in range(2):
+            to_twin(origin, h, act)
+
+    def sideways(pz, act, wait):
+        for d in range(1, nx):
+            origin = place(pz, y, around(x, d, nx))
+            if wait:
+                arrived(origin, 0)
+            to_y(origin, 0, act)
+            to_twin(origin, 0, act)
+        for d in range(1, ny):
+            origin = place(pz, around(y, d, ny), x)
+            if wait:
+                arrived(origin, 1)
+            to_x(origin, 1, act)
+            to_twin(origin, 1, act)
+
+    def last(pz, act, wait):
+        for d in range(1, ny):
+            for e in range(nx):
+                origin = place(pz, around(y, d, ny), around(x, e, nx))
+                if wait:
+                    arrived(origin, 0)
+                to_twin(origin, 0, act)
+        for d in range(1, nx):
+            for e in range(ny):
+                origin = place(pz, around(y, e, ny), around(x, d, nx))
+                if wait:
+                    arrived(origin, 1)
+                to_twin(origin, 1, act)
+
+    def above(pz, act):
+        @pl.when(z > 0)
+        def _():
+            for h in range(2):
+                act(copy(place(pz, y, x), h, send_z.at[0], place(z - 1, y, x)))
+
+    def below(pz, act):
+        @pl.when(z < nz - 1)
+        def _():
+            for h in range(2):
+                act(copy(place(pz, y, x), h, send_z.at[1], place(z + 1, y, x)))
+
+    mine = place(z, y, x)
+    above(z, start)
+    below(z, start)
+    spread(mine, start)
+
+    def first_wave(pz, onward):
+        origin = place(pz, y, x)
+        arrived(origin, 0)
+        arrived(origin, 1)
+        onward(pz, start)
+        spread(origin, start)
+
+    sideways(z, start, True)
+    for s in range(1, nz):
+        for pz, ok, onward in ((z - s, z - s >= 0, below), (z + s, z + s < nz, above)):
+            pl.when(ok)(functools.partial(first_wave, pz, onward))
+        for pz, ok in ((z - s, z - s >= 0), (z + s, z + s < nz)):
+            pl.when(ok)(functools.partial(sideways, pz, start, True))
+        if s == 1:
+            last(z, start, True)
+        else:
+            for pz, ok in ((z - s + 1, z - s + 1 >= 0), (z + s - 1, z + s - 1 < nz)):
+                pl.when(ok)(functools.partial(last, pz, start, True))
+    for pz, ok in ((z - nz + 1, z - nz + 1 >= 0), (z + nz - 1, z + nz - 1 < nz)):
+        pl.when(ok)(functools.partial(last, pz, start, True))
+
+    for b in range(dp):
+        for px in range(nx):
+            for h in range(2):
+                arrived((b, px * CORES + 1 - core), h)
+        for t in range(tp):
+            out_ref[b * rows:(b + 1) * rows, t * cols:(t + 1) * cols] = buf[b, t]
+
+    def ends(pz, onward=None):
+        if onward is not None:
+            onward(pz, ended)
+        spread(place(pz, y, x), ended)
+        sideways(pz, ended, False)
+        last(pz, ended, False)
+
+    above(z, ended)
+    below(z, ended)
+    ends(z)
+    for s in range(1, nz):
+        for pz, ok, onward in ((z - s, z - s >= 0, below), (z + s, z + s < nz, above)):
+            pl.when(ok)(functools.partial(ends, pz, onward))
+
+
+def full_gather(x, dp, tp, collective_id):
+    rows, cols = x.shape
+    nx = tp // CORES
+    ny = 2 ** (int(math.log2(dp)) // 2)
+    per_piece = (dp, nx, 2)
+    return pl.pallas_call(
+        functools.partial(full_gather_kernel, dp, ny, tp),
+        out_shape=jax.ShapeDtypeStruct((dp * rows, tp * cols), x.dtype),
+        in_specs=[pl.BlockSpec(memory_space=pltpu.VMEM)],
+        out_specs=pl.BlockSpec(memory_space=pltpu.VMEM),
+        scratch_shapes=[
+            pltpu.VMEM((dp, tp, rows, cols), x.dtype),
+            pltpu.SemaphoreType.DMA,
+            pltpu.SemaphoreType.DMA((2,) + per_piece),
+            pltpu.SemaphoreType.DMA((max(nx - 1, 1),) + per_piece),
+            pltpu.SemaphoreType.DMA((max(ny - 1, 1),) + per_piece),
+            pltpu.SemaphoreType.DMA(per_piece),
+            pltpu.SemaphoreType.DMA((dp, tp, 2)),
+        ],
+        compiler_params=pltpu.CompilerParams(
+            collective_id=collective_id, has_side_effects=True, vmem_limit_bytes=48 * 2**20),
+        cost_estimate=pl.CostEstimate(flops=0, bytes_accessed=rows * cols * dp * tp * 8, transcendentals=0),
+    )(x)
+
+
+def activate(mixed_in, ff_local):
+    gate_part = mixed_in[..., :ff_local]
+    up_part = mixed_in[..., ff_local:]
+    return (gate_part * jax.nn.sigmoid(glu_alpha * gate_part) * (up_part + 1.0)).astype(
+        jnp.bfloat16
     )
 
 
@@ -54,15 +331,14 @@
     q_local = w_query.shape[1] // head_size
     group_size = q_local // kv_local
     window = window_cache.shape[2]
-    attn_slice = lax.dynamic_slice_in_dim(attn_gain, col_start, col_count)
     moe_slice = lax.dynamic_slice_in_dim(moe_gain, col_start, col_count)
     tok_wide = tokens.astype(jnp.float32)
-    attn_sq = lax.psum(jnp.sum(tok_wide * tok_wide, axis=1), "tp")
-    normed = (
-        tok_wide * lax.rsqrt(attn_sq / full_width + norm_eps)[:, None] * attn_slice[None, :]
+    kv_flat = w_keyvalue.reshape(full_width, kv_local * 2 * head_size)
+    whole_rows = feature_gather(tokens, tp_count, 2, 0).astype(jnp.float32)
+    attn_sq = jnp.sum(whole_rows * whole_rows, axis=1, keepdims=True)
+    piece_rows = (
+        whole_rows * lax.rsqrt(attn_sq / full_width + norm_eps) * attn_gain[None, :]
     ).astype(jnp.bfloat16)
-    kv_flat = w_keyvalue.reshape(full_width, kv_local * 2 * head_size)
-    piece_rows = lax.all_gather(normed, "tp", axis=1, tiled=True)
     queries = jnp.dot(piece_rows, w_query, preferred_element_type=jnp.float32)
     fresh_rows = jnp.dot(piece_rows, kv_flat, preferred_element_type=jnp.float32)
     cosine, sine_table = rope_tables(positions, head_size)
@@ -114,6 +390,27 @@
     picked = jnp.sum(jnp.where(chosen, logits[:, None, :], 0.0), axis=-1)
     raised_logits = jnp.exp(picked)
     route_weights = raised_logits / jnp.sum(raised_logits, axis=1, keepdims=True)
+    gate_up_flat = gate_up.reshape(local_experts, full_width, 2 * ff_local)
+    if capacity >= seq_count:
+        token_weights = jnp.sum(jnp.where(chosen, route_weights[:, :, None], 0.0), axis=1)
+        all_rows = full_gather(hidden_rows, dp_count, tp_count, 1)
+        outs = []
+        for e in range(local_experts):
+            mixed_in = jnp.dot(all_rows, gate_up_flat[e], preferred_element_type=jnp.float32)
+            act_rows = activate(mixed_in, ff_local)
+            act_all = feature_gather(act_rows, tp_count, dp_count, 2 + e)
+            outs.append(
+                jnp.dot(act_all, w_down[e], preferred_element_type=jnp.float32).astype(jnp.bfloat16)
+            )
+        answered = jnp.stack(
+            [out.reshape(dp_count, seq_count, col_count) for out in outs], axis=1
+        )
+        returned = lax.all_to_all(answered, "dp", split_axis=0, concat_axis=0, tiled=True)
+        back = returned.reshape(experts, seq_count, col_count).astype(jnp.float32)
+        total = residual
+        for e in range(experts):
+            total = total + token_weights[:, e : e + 1] * back[e]
+        return total
     assign = expert_ids.reshape(-1)
     onehot = (assign[:, None] == expert_iota[None, :]).astype(jnp.int32)
     earlier = jnp.cumsum(onehot, axis=0) - onehot
@@ -123,7 +420,6 @@
     slot_hits = target[:, :, None] == spot_ids[None, None, :]
     placer = jnp.transpose(jnp.any(slot_hits, axis=1)).astype(jnp.bfloat16)
     combiner = jnp.sum(jnp.where(slot_hits, route_weights[:, :, None], 0.0), axis=1)
-    gate_up_flat = gate_up.reshape(local_experts, full_width, 2 * ff_local)
     placed = jnp.dot(placer, hidden_rows, preferred_element_type=jnp.float32).astype(jnp.bfloat16)
     mixed_in = jnp.einsum(
         "gecd,edf->gecf",
@@ -142,11 +438,7 @@
         gate_up_flat,
         preferred_element_type=jnp.float32,
     )
-    gate_part = mixed_in[..., :ff_local]
-    up_part = mixed_in[..., ff_local:]
-    act_rows = (gate_part * jax.nn.sigmoid(glu_alpha * gate_part) * (up_part + 1.0)).astype(
-        jnp.bfloat16
-    )
+    act_rows = activate(mixed_in, ff_local)
     answered = jnp.einsum(
         "gecf,efd->gecd",
         lax.all_gather(act_rows, "tp", axis=3, tiled=True),

time: 307 us -> 217 us (0.71)
  waiting for transfers between devices: 130 us -> 45.2 us
  Pallas kernels: 0 us -> 68.9 us
  blocking collectives: 61.2 us -> 13.1 us
  local copies, waits for them, and re-layouts: 46.1 us -> 26.7 us
  matrix products: 33.5 us -> 27.2 us
    all_gather x2 -> x0, waiting for transfers between devices: 86 us -> none  [the longest x1 44.3 us: on_device(): lax.all_gather(act_rows, 'tp', axis=3, tiled=True)]
    pallas_call x0 -> x3, Pallas kernels: none -> 68.9 us  [the longest x2 38.5 us: feature_gather(): pl.pallas_call(functools.partial(feature_gather_kernel, tp, chunks), out_...]
    all_to_all x1 -> x0, blocking collectives: 34.2 us -> none  [on_device(): lax.all_to_all(placed.reshape(dp_count, local_experts, capacity, hidden_r...]
    all_gather x3 -> x0, local copies, waits for them, and re-layouts: 17.2 us -> none  [the longest x1 8.35 us: on_device(): lax.all_gather(act_rows, 'tp', axis=3, tiled=True)]
    psum x1 -> x0, blocking collectives: 8.37 us -> none  [on_device(): attn_sq = lax.psum(jnp.sum(tok_wide * tok_wide, axis=1), 'tp')]
    all_gather x1 -> x0, blocking collectives: 6.68 us -> none  [on_device(): piece_rows = lax.all_gather(normed, 'tp', axis=1, tiled=True)]
    dot_general x4 -> x2, matrix products: 23.2 us -> 16.9 us  [the longest x1 10 us: on_device(): jnp.dot(all_rows, gate_up_flat[e], preferred_element_type=jnp.float32)]
    unnamed x28 -> x23, local copies, waits for them, and re-layouts: 14.7 us -> 12.9 us
  transfers between devices with their start and end apart: 4 -> 2, of which waited for: 4 -> 2; matrix products, arithmetic and copies ran while one was open for 1% -> 1% of each run, Pallas kernels for 0% -> 0%
where the time goes in v1:
time: 217 us; the launch traced here: 216 us
  Pallas kernels  68.9 us (32%)
  waiting for transfers between devices  45.2 us (21%)
  matrix products  27.2 us (13%)
  local copies, waits for them, and re-layouts  26.7 us (12%)
  other arithmetic  16.3 us (8%)
  between operations  13.6 us (6%)
  blocking collectives  13.1 us (6%)
  starting transfers between devices  4.41 us (2%)
    pallas_call x2, Pallas kernels, feature_gather(): pl.pallas_call(functools.partial(feature_gather_kernel, tp, chunks), out_...  38.5 us
    pallas_call x1, Pallas kernels, full_gather(): pl.pallas_call(functools.partial(full_gather_kernel, dp, ny, tp), out_sha...  30.4 us
    unnamed x2, waiting for transfers between devices  23.3 us
    all_to_all x1, waiting for transfers between devices, on_device(): lax.all_to_all(answered, 'dp', split_axis=0, concat_axis=0, tiled=True)  21.9 us
    unnamed x23, local copies, waits for them, and re-layouts  12.9 us
    dot_general x1, matrix products, on_device(): jnp.dot(all_rows, gate_up_flat[e], preferred_element_type=jnp.float32)  10 us
    select_n x1, other arithmetic, on_device(): jnp.where(is_current[:, None, :, None], new_entry[:, :, None, :], window_...  7.16 us
    psum x1, blocking collectives, on_device(): lax.psum(jnp.dot(scaled, router_wide, precision=lax.Precision.HIGHEST), '...  7.15 us
  transfers between devices with their start and end apart: 2, of which 2 were waited for; matrix products, arithmetic and copies ran while one was open for 1% of the time, Pallas kernels for 0%

profile of v1, /device:TPU:0, one launch (start us, length us, event | category | flops | bytes accessed | tf_op | source)
XLA Modules:
  0.0 215.5 jit_solution(7114323355059772657)
XLA Ops:
  7.4 1.4 fusion.56
  12.7 8.7 %shard_map.127 = bf16[96,2880]{1,0:T(8,128)(2,1)S(1)} custom-call(bf16[96,720]{1,0:T(8,128)(2,1)S(1)} %copy-done.1), custom_call_target="tpu_custom_call" | custom-call | bytes 4423680 | tf_op jit(solution)/shard_map/pallas_call | solution.py:109
  21.6 3.2 %fusion.51 = f32[96,512]{0,1:T(8,128)S(1)} fusion(bf16[2880,512]{1,0:T(8,128)(2,1)} %param.15, bf16[96,2880]{1,0:T(8,128)(2,1)S(1)} %shard_map.127, f32[2880]{0:T(1024)} %param.14, f32[96]{0:T(128)S(1)} %add_rsqrt_fusion.1), kind=kOutput, calls=%fused_computation.60 | convolution fusion | flops 284221440 | bytes 3710592 | tf_op jit(solution)/shard_map/dot_general | solution.py:342
  25.4 1.7 copy.65
  27.1 1.7 copy.66
  28.8 4.9 %copy.82 = bf16[2880,2,128]{0,2,1:T(8,128)(2,1)} copy(bf16[2880,2,128]{2,1,0:T(2,128)(2,1)} %param.16) | data formatting | bytes 2949120 | tf_op jit(solution)/shard_map/dot_general | solution.py:343
  33.6 2.0 fusion.11
  36.8 8.7 %copy.72 = bf16[96,2,128,128]{2,3,1,0:T(8,128)(2,1)} copy(bf16[96,2,128,128]{3,2,1,0:T(8,128)(2,1)} %param.19) | data formatting | bytes 12582912 | tf_op args[6]
  45.5 7.2 %broadcast_select_fusion = bf16[96,2,128,128]{2,3,1,0:T(8,128)(2,1)S(1)} fusion(bf16[96,2,128,128]{2,3,1,0:T(8,128)(2,1)} %copy.72, pred[96,128]{1,0:T(8,128)(4,1)S(1)} %copy-done.5, bf16[96,2,128]{2,1,0:T(2,128)(2,1)S(1)} %copy.71), kind=kLoop, calls=%fused_computation | loop fusion | flops 3145728 | bytes 12644352 | tf_op jit(solution)/shard_map/jit(_where)/select_n | solution.py:355
  52.7 1.2 fusion.63
  54.6 1.8 fusion.19
  56.6 1.9 convolution_convert_fusion
  58.5 2.2 %copy.83 = bf16[96,2880]{0,1:T(8,128)(2,1)} copy(bf16[96,2880]{1,0:T(8,128)(2,1)} %convolution_convert_fusion) | data formatting | bytes 1105920
  61.5 23.2 %reduce-scatter.4.cloned.1.call-done = bf16[720,96]{1,0:T(8,128)(2,1)} async-done(((bf16[2880,96]{1,0:T(8,128)(2,1)}), bf16[720,96]{1,0:T(8,128)(2,1)}) %reduce-scatter.4.cloned.1.call-update) | async-done | bytes 138256
  86.0 5.9 %psum.14 = f32[96]{0:T(128)S(1)} all-reduce(f32[96]{0:T(128)S(1)} %multiply_reduce_fusion), channel_id=1, replica_groups=mesh['dp'=8,'tp'=4] {'tp'}, use_global_device_ids=true, to_apply=%region_5.6 | all-reduce | flops 96 | bytes 768 | tf_op jit(solution)/shard_map/psum | solution.py:383
  92.0 30.4 %shard_map.128 = bf16[768,2880]{1,0:T(8,128)(2,1)S(1)} custom-call(bf16[96,720]{1,0:T(8,128)(2,1)S(1)} %fusion.43.x_ref), custom_call_target="tpu_custom_call" | custom-call | bytes 17694720 | tf_op jit(solution)/shard_map/pallas_call | solution.py:281
  122.4 10.0 %fusion.64 = f32[768,1440]{1,0:T(8,128)S(1)} fusion(bf16[768,2880]{1,0:T(8,128)(2,1)S(1)} %shard_map.128, bf16[2880,1440]{0,1:T(8,128)(2,1)} %bitcast.130), kind=kOutput, calls=%fused_computation.105 | convolution fusion | flops 6370099200 | bytes 17141760 | tf_op jit(solution)/shard_map/dot_general | solution.py:399
  133.3 29.9 %shard_map.129 = bf16[768,2880]{1,0:T(8,128)(2,1)S(1)} custom-call(bf16[768,720]{1,0:T(8,128)(2,1)S(1)} %fusion.7.x_ref), custom_call_target="tpu_custom_call" | custom-call | bytes 35389440 | tf_op jit(solution)/shard_map/pallas_call | solution.py:109
  163.1 6.9 %fusion.8 = bf16[768,720]{0,1:T(8,128)(2,1)} fusion(bf16[768,2880]{1,0:T(8,128)(2,1)S(1)} %shard_map.129, bf16[1,2880,720]{1,2,0:T(8,128)(2,1)} %param.24), kind=kOutput, calls=%fused_computation.11 | convolution fusion | flops 3185602560 | bytes 9676800 | tf_op jit(solution)/shard_map/dot_general | solution.py:403
  170.0 2.4 %copy.76 = bf16[768,720]{1,0:T(8,128)(2,1)} copy(bf16[768,720]{0,1:T(8,128)(2,1)} %fusion.8) | data formatting | bytes 2211840 | tf_op jit(solution)/shard_map/convert_element_type | solution.py:403
  172.4 4.4 %all-to-all-start = ((bf16[8,1,96,720]{3,2,1,0:T(8,128)(2,1)}), bf16[8,1,96,720]{3,2,1,0:T(8,128)(2,1)}, u32[]{:S(2)}, u32[]{:S(2)}) async-start(bf16[8,1,96,720]{3,2,1,0:T(8,128)(2,1)} %bitcast.115), calls=%async_computation | async-start | bytes 2359296 | tf_op jit(solution)/shard_map/all_to_all | solution.py:408
  177.1 7.2 %psum.15 = f32[96,8]{0,1:T(8,128)S(1)} all-reduce(f32[96,8]{0,1:T(8,128)S(1)} %fusion.44), channel_id=1, replica_groups=mesh['dp'=8,'tp'=4] {'tp'}, use_global_device_ids=true, to_apply=%region_6.7 | all-reduce | flops 768 | bytes 6144 | tf_op jit(solution)/shard_map/psum | solution.py:386
  184.3 21.9 %all-to-all-done = bf16[8,1,96,720]{3,2,1,0:T(8,128)(2,1)} async-done(((bf16[8,1,96,720]{3,2,1,0:T(8,128)(2,1)}), bf16[8,1,96,720]{3,2,1,0:T(8,128)(2,1)}, u32[]{:S(2)}, u32[]{:S(2)}) %all-to-all-start) | async-done | bytes 1105952 | tf_op jit(solution)/shard_map/all_to_all | solution.py:408
  206.2 1.5 convert_element_type.56
  (53 shorter events, 11.8 us)
Async XLA Ops:
  6.5 50.1 %copy-start = (bf16[512,2880]{0,1:T(8,128)(2,1)S(1)}, bf16[512,2880]{0,1:T(8,128)(2,1)}, u32[]{:S(2)}) copy-start(bf16[512,2880]{0,1:T(8,128)(2,1)} %param.18) | copy-start | bytes 8847364
  6.5 78.2 %reduce-scatter.4.cloned.1.call-start = ((), (), s32[]{:S(2)}) async-start(), calls=%async_computation.2 | async-start | bytes 921600
  11.8 0.9 copy-start.1
  36.8 8.7 %copy-start.5 = (pred[96,128]{1,0:T(8,128)(4,1)S(1)}, pred[96,128]{1,0:T(8,128)(4,1)}, u32[]{:S(2)}) copy-start(pred[96,128]{1,0:T(8,128)(4,1)} %iota_compare_fusion) | copy-start | bytes 36868
  45.5 7.2 %copy-start.3 = (bf16[96,8,32]{2,1,0:T(8,128)(2,1)S(1)}, bf16[96,8,32]{2,1,0:T(8,128)(2,1)}, u32[]{:S(2)}) copy-start(bf16[96,8,32]{2,1,0:T(8,128)(2,1)} %copy.65) | copy-start | bytes 147460
  45.5 7.2 %copy-start.4 = (bf16[96,8,32]{2,1,0:T(8,128)(2,1)S(1)}, bf16[96,8,32]{2,1,0:T(8,128)(2,1)}, u32[]{:S(2)}) copy-start(bf16[96,8,32]{2,1,0:T(8,128)(2,1)} %copy.66) | copy-start | bytes 147460
  45.5 7.2 %copy-start.6 = (pred[96,128]{1,0:T(8,128)(4,1)S(1)}, pred[96,128]{1,0:T(8,128)(4,1)}, u32[]{:S(2)}) copy-start(pred[96,128]{1,0:T(8,128)(4,1)} %fusion.56) | copy-start | bytes 36868
  56.6 29.2 %copy-start.2 = (bf16[96,720]{1,0:T(8,128)(2,1)S(1)}, bf16[96,720]{1,0:T(8,128)(2,1)}, u32[]{:S(2)}) copy-start(bf16[96,720]{1,0:T(8,128)(2,1)} %x_ref.1) | copy-start | bytes 414724
  170.0 6.8 %copy-start.8 = (bf16[720,8]{0,1:T(8,128)(2,1)S(1)}, bf16[720,8]{0,1:T(8,128)(2,1)}, u32[]{:S(2)}) copy-start(bf16[720,8]{0,1:T(8,128)(2,1)} %param.22) | copy-start | bytes 34564
  170.0 14.3 %copy-start.7 = (s32[96,4]{0,1:T(4,128)S(1)}, s32[96,4]{0,1:T(4,128)}, u32[]{:S(2)}) copy-start(s32[96,4]{0,1:T(4,128)} %param.25) | copy-start | bytes 4612
  172.4 33.9 %all-to-all-start = ((bf16[8,1,96,720]{3,2,1,0:T(8,128)(2,1)}), bf16[8,1,96,720]{3,2,1,0:T(8,128)(2,1)}, u32[]{:S(2)}, u32[]{:S(2)}) async-start(bf16[8,1,96,720]{3,2,1,0:T(8,128)(2,1)} %bitcast.115), calls=%async_computation | async-start | bytes 2359296 | tf_op jit(solution)/shard_map/all_to_all | solution.py:408
Sparse Core Ops, SparseCore 0:
  60.9 23.8 reduce-scatter.3

commit v2 on v1

--- a/solution.py
+++ b/solution.py
@@ -124,6 +124,52 @@
     )(x)
 
 
+def share_sum_kernel(tp, scatter, x_ref, out_ref, buf, send_sem, recv_sem):
+    chips = tp // CORES
+    dp_id = lax.axis_index("dp")
+    me = lax.axis_index("tp")
+    core = lax.rem(me, CORES)
+    chip = me // CORES
+    others = [
+        lax.rem(chip + d, chips) * CORES + c for d in range(1, chips) for c in range(CORES)
+    ] + [chip * CORES + (1 - core)]
+    greet([(dp_id, other) for other in others])
+    sent = []
+    for i, other in enumerate(others):
+        sent.append(pltpu.make_async_remote_copy(
+            src_ref=x_ref.at[other if scatter else 0], dst_ref=buf.at[me], send_sem=send_sem.at[i],
+            recv_sem=recv_sem.at[me], device_id=(dp_id, other), device_id_type=MESH))
+        sent[-1].start()
+    total = x_ref[me if scatter else 0].astype(jnp.float32)
+    for i in reversed(range(len(others))):
+        other = others[i]
+        pltpu.make_async_remote_copy(
+            src_ref=buf.at[other], dst_ref=buf.at[other], send_sem=send_sem.at[i],
+            recv_sem=recv_sem.at[other], device_id=(dp_id, other), device_id_type=MESH).wait_recv()
+        total = total + buf[other].astype(jnp.float32)
+    out_ref[...] = total
+    for copy in sent:
+        copy.wait_send()
+
+
+def share_sum(x, tp, scatter, collective_id):
+    rows, cols = x.shape[1:]
+    return pl.pallas_call(
+        functools.partial(share_sum_kernel, tp, scatter),
+        out_shape=jax.ShapeDtypeStruct((rows, cols), jnp.float32),
+        in_specs=[pl.BlockSpec(memory_space=pltpu.VMEM)],
+        out_specs=pl.BlockSpec(memory_space=pltpu.VMEM),
+        scratch_shapes=[
+            pltpu.VMEM((tp, rows, cols), x.dtype),
+            pltpu.SemaphoreType.DMA((tp - 1,)),
+            pltpu.SemaphoreType.DMA((tp,)),
+        ],
+        compiler_params=pltpu.CompilerParams(
+            collective_id=collective_id, has_side_effects=True, vmem_limit_bytes=16 * 2**20),
+        cost_estimate=pl.CostEstimate(flops=0, bytes_accessed=rows * cols * tp * 16, transcendentals=0),
+    )(x)
+
+
 def full_gather_kernel(dp, ny, tp, x_ref, out_ref, buf, own_sem, send_z, send_x, send_y, send_c, recv):
     nz, nx = dp // ny, tp // CORES
     dp_id = lax.axis_index("dp")
@@ -255,8 +301,12 @@
         for px in range(nx):
             for h in range(2):
                 arrived((b, px * CORES + 1 - core), h)
-        for t in range(tp):
-            out_ref[b * rows:(b + 1) * rows, t * cols:(t + 1) * cols] = buf[b, t]
+        for h in range(2):
+            start_row = (h * dp + b) * half
+            for t in range(tp):
+                out_ref[start_row:start_row + half, t * cols:(t + 1) * cols] = buf[
+                    b, t, h * half:(h + 1) * half
+                ]
 
     def ends(pz, onward=None):
         if onward is not None:
@@ -352,27 +402,39 @@
     )
     slot_ids = jnp.arange(window, dtype=jnp.int32)
     is_current = slot_ids[None, :] == (positions % window)[:, None]
-    cache_now = jnp.where(is_current[:, None, :, None], new_entry[:, :, None, :], window_cache)
     is_valid = (positions[:, None] - slot_ids[None, :]) % window <= positions[:, None]
+    is_valid = is_valid & ~is_current
     grouped = rot_queries.reshape(seq_count, kv_local, group_size, head_size)
     scores = jnp.einsum(
-        "skgh,skwh->skgw", grouped, cache_now[..., :head_size], preferred_element_type=jnp.float32
+        "skgh,skwh->skgw", grouped, window_cache[..., :head_size], preferred_element_type=jnp.float32
     ) * head_size ** (-0.5)
     scores = jnp.where(is_valid[:, None, None, :], scores, -jnp.inf)
+    new_wide = new_entry.astype(jnp.float32)[:, :, None, :]
+    new_score = jnp.sum(
+        grouped.astype(jnp.float32) * new_wide[..., :head_size], axis=-1, keepdims=True
+    ) * head_size ** (-0.5)
     sink_col = attn_sinks.reshape(kv_local, group_size)[None, :, :, None]
-    peak_score = jnp.maximum(jnp.max(scores, axis=-1, keepdims=True), sink_col)
+    peak_score = jnp.maximum(
+        jnp.maximum(jnp.max(scores, axis=-1, keepdims=True), new_score), sink_col
+    )
     raised = jnp.exp(scores - peak_score)
-    denominator = jnp.sum(raised, axis=-1, keepdims=True) + jnp.exp(sink_col - peak_score)
+    raised_new = jnp.exp(new_score - peak_score)
+    denominator = (
+        jnp.sum(raised, axis=-1, keepdims=True) + raised_new + jnp.exp(sink_col - peak_score)
+    )
     prob_bf = (raised / denominator).astype(jnp.bfloat16)
+    prob_new = (raised_new / denominator).astype(jnp.bfloat16).astype(jnp.float32)
     attended = jnp.einsum(
-        "skgw,skwh->skgh", prob_bf, cache_now[..., head_size:], preferred_element_type=jnp.float32
+        "skgw,skwh->skgh", prob_bf, window_cache[..., head_size:], preferred_element_type=jnp.float32
+    )
+    attended = (attended + prob_new * new_wide[..., head_size:]).astype(jnp.bfloat16)
+    partial_out = jnp.einsum(
+        "sh,htc->tsc",
+        attended.reshape(seq_count, q_local * head_size),
+        w_out.reshape(q_local * head_size, tp_count, col_count),
+        preferred_element_type=jnp.float32,
     ).astype(jnp.bfloat16)
-    partial_out = jnp.dot(
-        attended.reshape(seq_count, q_local * head_size), w_out, preferred_element_type=jnp.float32
-    )
-    residual = tok_wide + lax.psum_scatter(
-        partial_out.astype(jnp.bfloat16), "tp", scatter_dimension=1, tiled=True
-    ).astype(jnp.float32)
+    residual = tok_wide + share_sum(partial_out, tp_count, True, 2)
     experts = router.shape[1]
     top_count = expert_ids.shape[1]
     local_experts = gate_up.shape[0]
@@ -380,11 +442,14 @@
     capacity = min(seq_count, max(2, 8 * seq_count * top_count // (3 * experts)))
     moe_sq = jnp.sum(residual * residual, axis=1)
     router_wide = router.astype(jnp.float32)
-    total_sq = lax.psum(moe_sq, "tp")
-    moe_scale = lax.rsqrt(total_sq / full_width + norm_eps)[:, None]
-    scaled = residual * moe_scale * moe_slice[None, :]
-    logits = lax.psum(jnp.dot(scaled, router_wide, precision=lax.Precision.HIGHEST), "tp")
-    hidden_rows = scaled.astype(jnp.bfloat16)
+    gained = residual * moe_slice[None, :]
+    raw_logits = jnp.dot(gained, router_wide, precision=lax.Precision.HIGHEST)
+    stats = share_sum(
+        jnp.concatenate([moe_sq[:, None], raw_logits], axis=1)[None], tp_count, False, 3
+    )
+    moe_scale = lax.rsqrt(stats[:, :1] / full_width + norm_eps)
+    logits = stats[:, 1:] * moe_scale
+    hidden_rows = (gained * moe_scale).astype(jnp.bfloat16)
     expert_iota = jnp.arange(experts, dtype=jnp.int32)
     chosen = expert_ids[:, :, None] == expert_iota[None, None, :]
     picked = jnp.sum(jnp.where(chosen, logits[:, None, :], 0.0), axis=-1)
@@ -394,22 +459,33 @@
     if capacity >= seq_count:
         token_weights = jnp.sum(jnp.where(chosen, route_weights[:, :, None], 0.0), axis=1)
         all_rows = full_gather(hidden_rows, dp_count, tp_count, 1)
-        outs = []
-        for e in range(local_experts):
-            mixed_in = jnp.dot(all_rows, gate_up_flat[e], preferred_element_type=jnp.float32)
-            act_rows = activate(mixed_in, ff_local)
-            act_all = feature_gather(act_rows, tp_count, dp_count, 2 + e)
-            outs.append(
-                jnp.dot(act_all, w_down[e], preferred_element_type=jnp.float32).astype(jnp.bfloat16)
+        half = seq_count // 2
+        part = dp_count * half
+        acts = [
+            activate(
+                jnp.dot(all_rows, gate_up_flat[e], preferred_element_type=jnp.float32), ff_local
             )
-        answered = jnp.stack(
-            [out.reshape(dp_count, seq_count, col_count) for out in outs], axis=1
-        )
-        returned = lax.all_to_all(answered, "dp", split_axis=0, concat_axis=0, tiled=True)
-        back = returned.reshape(experts, seq_count, col_count).astype(jnp.float32)
-        total = residual
-        for e in range(experts):
-            total = total + token_weights[:, e : e + 1] * back[e]
+            for e in range(local_experts)
+        ]
+        pieces = []
+        for h in range(2):
+            outs = []
+            for e in range(local_experts):
+                act_all = feature_gather(
+                    acts[e][h * part : (h + 1) * part], tp_count, dp_count // 2, 4 + 2 * e + h
+                )
+                out = jnp.dot(act_all, w_down[e], preferred_element_type=jnp.float32)
+                outs.append(out.astype(jnp.bfloat16).reshape(dp_count, half, col_count))
+            returned = lax.all_to_all(
+                jnp.stack(outs, axis=1), "dp", split_axis=0, concat_axis=0, tiled=True
+            )
+            back = returned.reshape(experts, half, col_count)
+            mine = slice(h * half, (h + 1) * half)
+            total = residual[mine]
+            for e in range(experts):
+                total = total + token_weights[mine, e : e + 1] * back[e].astype(jnp.float32)
+            pieces.append(total)
+        total = jnp.concatenate(pieces, axis=0)
         return total
     assign = expert_ids.reshape(-1)
     onehot = (assign[:, None] == expert_iota[None, :]).astype(jnp.int32)

time: 217 us -> 193 us (0.89)
  waiting for transfers between devices: 45.2 us -> 15.2 us
  Pallas kernels: 68.9 us -> 87.2 us
  matrix products: 27.2 us -> 41.4 us
  between operations: 13.6 us -> 0.31 us
  blocking collectives: 13.1 us -> 0 us
  starting transfers between devices: 4.41 us -> 10.4 us
  other arithmetic: 16.3 us -> 12.9 us
  local copies, waits for them, and re-layouts: 26.7 us -> 24 us
    unnamed x2 -> x0, waiting for transfers between devices: 23.3 us -> none
    dot_general x5 -> x6, matrix products: 12.1 us -> 25.9 us  [the longest x2 10.9 us: on_device(): out = jnp.dot(act_all, w_down[e], preferred_element_type=jnp.float32)]
    pallas_call x0 -> x2, Pallas kernels: none -> 13.6 us  [share_sum(): pl.pallas_call(functools.partial(share_sum_kernel, tp, scatter), out_shap...]
    psum x2 -> x0, blocking collectives: 13.1 us -> none  [the longest x1 7.15 us: on_device(): lax.psum(jnp.dot(scaled, router_wide, precision=lax.Precision.HIGHEST), '...]
    unnamed x23 -> x26, local copies, waits for them, and re-layouts: 12.9 us -> 1.45 us
    select_n x1 -> x0, other arithmetic: 7.16 us -> none  [on_device(): jnp.where(is_current[:, None, :, None], new_entry[:, :, None, :], window_...]
    all_to_all x1 -> x2, waiting for transfers between devices: 21.9 us -> 15.2 us  [on_device(): lax.all_to_all(jnp.stack(outs, axis=1), 'dp', split_axis=0, concat_axis=0...]
    all_to_all x1 -> x2, starting transfers between devices: 4.41 us -> 10.4 us  [on_device(): lax.all_to_all(jnp.stack(outs, axis=1), 'dp', split_axis=0, concat_axis=0...]
  transfers between devices with their start and end apart: 2 -> 2, of which waited for: 2 -> 1; matrix products, arithmetic and copies ran while one was open for 1% -> 6% of each run, Pallas kernels for 0% -> 9%
where the time goes in v2:
time: 193 us; the launch traced here: 192 us
  Pallas kernels  87.2 us (45%)
  matrix products  41.4 us (21%)
  local copies, waits for them, and re-layouts  24 us (12%)
  waiting for transfers between devices  15.2 us (8%)
  other arithmetic  12.9 us (7%)
  starting transfers between devices  10.4 us (5%)
    pallas_call x3, Pallas kernels, feature_gather(): pl.pallas_call(functools.partial(feature_gather_kernel, tp, chunks), out_...  42.3 us
    pallas_call x1, Pallas kernels, full_gather(): pl.pallas_call(functools.partial(full_gather_kernel, dp, ny, tp), out_sha...  31.3 us
    all_to_all x2, waiting for transfers between devices, on_device(): lax.all_to_all(jnp.stack(outs, axis=1), 'dp', split_axis=0, concat_axis=0...  15.2 us
    pallas_call x2, Pallas kernels, share_sum(): pl.pallas_call(functools.partial(share_sum_kernel, tp, scatter), out_shap...  13.6 us
    dot_general x2, matrix products, on_device(): out = jnp.dot(act_all, w_down[e], preferred_element_type=jnp.float32)  10.9 us
    all_to_all x2, starting transfers between devices, on_device(): lax.all_to_all(jnp.stack(outs, axis=1), 'dp', split_axis=0, concat_axis=0...  10.4 us
    dot_general x1, matrix products, on_device(): jnp.dot(all_rows, gate_up_flat[e], preferred_element_type=jnp.float32)  10.2 us
    dot_general x1, matrix products, on_device(): jnp.einsum('skgh,skwh->skgw', grouped, window_cache[..., :head_size], pre...  7.85 us
  transfers between devices with their start and end apart: 2, of which 1 were waited for; matrix products, arithmetic and copies ran while one was open for 6% of the time, Pallas kernels for 9%

profile of v2, /device:TPU:0, one launch (start us, length us, event | category | flops | bytes accessed | tf_op | source)
XLA Modules:
  0.0 191.5 jit_solution(7331570918606781942)
XLA Ops:
  1.6 1.4 fusion.66
  5.5 8.7 %shard_map.127 = bf16[96,2880]{1,0:T(8,128)(2,1)S(1)} custom-call(bf16[96,720]{1,0:T(8,128)(2,1)S(1)} %copy-done.1), custom_call_target="tpu_custom_call" | custom-call | bytes 4423680 | tf_op jit(solution)/shard_map/pallas_call | solution.py:109
  14.4 3.2 %fusion.41 = f32[96,512]{0,1:T(8,128)S(1)} fusion(bf16[2880,512]{1,0:T(8,128)(2,1)} %param.15, bf16[96,2880]{1,0:T(8,128)(2,1)S(1)} %shard_map.127, f32[2880]{0:T(1024)} %param.14, f32[96]{0:T(128)S(1)} %add_rsqrt_fusion), kind=kOutput, calls=%fused_computation.40 | convolution fusion | flops 284221440 | bytes 3710592 | tf_op jit(solution)/shard_map/dot_general | solution.py:392
  18.2 1.7 copy.107
  19.9 1.7 copy.108
  21.6 7.8 %fusion.72 = (f32[96,2,4]{2,1,0:T(2,128)}, f32[96,2,4,128]{3,2,1,0:T(4,128)}) fusion(bf16[96,2,128,128]{3,2,1,0:T(8,128)(2,1)} %param.19, bf16[96,2,4,32]{3,2,1,0:T(4,128)(2,1)} %bitcast.170, bf16[96,2,4,32]{3,2,1,0:T(4,128)(2,1)} %bitcast.168, pred[96,128]{1,0:T(8,128)(4,1)} %fusion.66), kind=kOutput, calls=%fused_computation.151 | convolution fusion | flops 13073664 | bytes 6798336 | tf_op jit(solution)/shard_map/skgh,skwh->skgw/dot_general | solution.py:408
  30.4 4.9 %copy.138 = bf16[2880,2,128]{0,2,1:T(8,128)(2,1)} copy(bf16[2880,2,128]{2,1,0:T(2,128)(2,1)} %param.16) | data formatting | bytes 2949120 | tf_op jit(solution)/shard_map/dot_general | solution.py:393
  35.3 2.0 %fusion.10 = f32[96,2,128]{2,0,1:T(8,128)S(1)} fusion(bf16[2880,2,128]{0,2,1:T(8,128)(2,1)} %copy.138, bf16[96,2880]{1,0:T(8,128)(2,1)S(1)} %shard_map.127, f32[2880]{0:T(1024)S(1)} %copy-done.9, f32[96]{0:T(128)S(1)} %add_rsqrt_fusion), kind=kOutput, calls=%fused_computation.11 | convolution fusion | flops 142663680 | bytes 2137728 | tf_op jit(solution)/shard_map/dot_general | solution.py:393
  40.9 1.4 fusion.68
  44.9 5.9 %fusion.25 = bf16[96,2,4,64]{3,2,1,0:T(4,128)(2,1)} fusion(bf16[96,2,128,128]{3,2,1,0:T(8,128)(2,1)} %param.19, f32[96,2,4,128]{3,2,1,0:T(4,128)S(1)} %copy-done.8, f32[96,2,64]{2,1,0:T(2,128)S(1)} %copy.122, f32[96,2,4]{2,1,0:T(2,128)S(1)} %copy.121, f32[96,2,4]{2,1,0:T(2,128)} %copy.119, f32[96,2,4]{2,1,0:T(2,128)S(1)} %copy.117), kind=kOutput, calls=%fused_computation.21 | convolution fusion | flops 13025280 | bytes 6841344 | tf_op jit(solution)/shard_map/skgw,skwh->skgh/dot_general | solution.py:427
  52.9 8.1 %shard_map.128 = f32[96,720]{1,0:T(8,128)S(1)} custom-call(bf16[4,96,720]{2,1,0:T(8,128)(2,1)S(1)} %fusion.18.x_ref), custom_call_target="tpu_custom_call" | custom-call | bytes 4423680 | tf_op jit(solution)/shard_map/pallas_call | solution.py:157
  62.4 5.5 %shard_map.129 = f32[96,9]{1,0:T(8,128)S(1)} custom-call(f32[1,96,9]{2,1,0:T(8,128)S(1)} %bitcast.164), custom_call_target="tpu_custom_call" | custom-call | bytes 55296 | tf_op jit(solution)/shard_map/pallas_call | solution.py:157
  68.6 31.3 %shard_map.130 = bf16[768,2880]{1,0:T(8,128)(2,1)S(1)} custom-call(bf16[96,720]{1,0:T(8,128)(2,1)S(1)} %multiply_convert_fusion.x_ref), custom_call_target="tpu_custom_call" | custom-call | bytes 17694720 | tf_op jit(solution)/shard_map/pallas_call | solution.py:331
  99.9 10.2 %fusion.73 = f32[768,1440]{1,0:T(8,128)S(1)} fusion(bf16[768,2880]{1,0:T(8,128)(2,1)S(1)} %shard_map.130, bf16[2880,1440]{0,1:T(8,128)(2,1)} %bitcast.174), kind=kOutput, calls=%fused_computation.152 | convolution fusion | flops 6370099200 | bytes 17141760 | tf_op jit(solution)/shard_map/dot_general | solution.py:466
  111.1 16.8 %shard_map.131 = bf16[384,2880]{1,0:T(8,128)(2,1)S(1)} custom-call(bf16[384,720]{1,0:T(8,128)(2,1)S(1)} %get-tuple-element.9.x_ref), custom_call_target="tpu_custom_call" | custom-call | bytes 17694720 | tf_op jit(solution)/shard_map/pallas_call | solution.py:109
  127.9 5.5 %fusion.12 = bf16[384,720]{0,1:T(8,128)(2,1)} fusion(bf16[384,2880]{1,0:T(8,128)(2,1)S(1)} %shard_map.131, bf16[1,2880,720]{1,2,0:T(8,128)(2,1)} %param.24), kind=kOutput, calls=%fused_computation.16 | convolution fusion | flops 1592801280 | bytes 6912000 | tf_op jit(solution)/shard_map/dot_general | solution.py:477
  133.4 2.1 %copy.130 = bf16[384,720]{1,0:T(8,128)(2,1)} copy(bf16[384,720]{0,1:T(8,128)(2,1)} %fusion.12) | data formatting | bytes 1105920 | tf_op jit(solution)/shard_map/convert_element_type | solution.py:478
  135.5 4.7 %all-to-all-start = ((bf16[8,1,48,720]{3,2,1,0:T(8,128)(2,1)}), bf16[8,1,48,720]{3,2,1,0:T(8,128)(2,1)}, u32[]{:S(2)}, u32[]{:S(2)}) async-start(bf16[8,1,48,720]{3,2,1,0:T(8,128)(2,1)} %bitcast.166), calls=%async_computation | async-start | bytes 1179648 | tf_op jit(solution)/shard_map/all_to_all | solution.py:479
  140.2 1.5 slice_multiply_fusion
  142.5 16.8 %shard_map.132 = bf16[384,2880]{1,0:T(8,128)(2,1)S(1)} custom-call(bf16[384,720]{1,0:T(8,128)(2,1)S(1)} %get-tuple-element.10.x_ref), custom_call_target="tpu_custom_call" | custom-call | bytes 17694720 | tf_op jit(solution)/shard_map/pallas_call | solution.py:109
  159.3 5.5 %fusion.15 = bf16[384,720]{0,1:T(8,128)(2,1)} fusion(bf16[384,2880]{1,0:T(8,128)(2,1)S(1)} %shard_map.132, bf16[1,2880,720]{1,2,0:T(8,128)(2,1)} %param.24), kind=kOutput, calls=%fused_computation.17 | convolution fusion | flops 1592801280 | bytes 6912000 | tf_op jit(solution)/shard_map/dot_general | solution.py:477
  164.8 2.2 %copy.131 = bf16[384,720]{1,0:T(8,128)(2,1)} copy(bf16[384,720]{0,1:T(8,128)(2,1)} %fusion.15) | data formatting | bytes 1105920 | tf_op jit(solution)/shard_map/convert_element_type | solution.py:478
  167.0 5.7 %all-to-all-start.1 = ((bf16[8,1,48,720]{3,2,1,0:T(8,128)(2,1)}), bf16[8,1,48,720]{3,2,1,0:T(8,128)(2,1)}, u32[]{:S(2)}, u32[]{:S(2)}) async-start(bf16[8,1,48,720]{3,2,1,0:T(8,128)(2,1)} %bitcast.165), calls=%async_computation.1 | async-start | bytes 1179648 | tf_op jit(solution)/shard_map/all_to_all | solution.py:479
  174.2 15.2 %all-to-all-done.1 = bf16[8,1,48,720]{3,2,1,0:T(8,128)(2,1)} async-done(((bf16[8,1,48,720]{3,2,1,0:T(8,128)(2,1)}), bf16[8,1,48,720]{3,2,1,0:T(8,128)(2,1)}, u32[]{:S(2)}, u32[]{:S(2)}) %all-to-all-start.1) | async-done | bytes 552992 | tf_op jit(solution)/shard_map/all_to_all | solution.py:479
  (71 shorter events, 21.4 us)
Async XLA Ops:
  0.0 51.9 %copy-start = (bf16[512,2880]{0,1:T(8,128)(2,1)S(1)}, bf16[512,2880]{0,1:T(8,128)(2,1)}, u32[]{:S(2)}) copy-start(bf16[512,2880]{0,1:T(8,128)(2,1)} %param.18) | copy-start | bytes 8847364
  0.9 39.1 %copy-start.12 = (f32[2,4]{1,0:T(2,128)}, f32[2,4]{1,0:T(2,128)S(1)}, u32[]{:S(2)}) copy-start(f32[2,4]{1,0:T(2,128)S(1)} %max.36) | copy-start | bytes 100
  4.6 0.9 copy-start.1
  29.4 5.9 %copy-start.9 = (f32[2880]{0:T(1024)S(1)}, f32[2880]{0:T(1024)}, u32[]{:S(2)}) copy-start(f32[2880]{0:T(1024)} %param.14) | copy-start | bytes 34564
  35.3 4.0 %copy-start.6 = (bf16[96,8,32]{2,1,0:T(8,128)(2,1)S(1)}, bf16[96,8,32]{2,1,0:T(8,128)(2,1)}, u32[]{:S(2)}) copy-start(bf16[96,8,32]{2,1,0:T(8,128)(2,1)} %copy.107) | copy-start | bytes 147460
  35.3 4.0 %copy-start.7 = (bf16[96,8,32]{2,1,0:T(8,128)(2,1)S(1)}, bf16[96,8,32]{2,1,0:T(8,128)(2,1)}, u32[]{:S(2)}) copy-start(bf16[96,8,32]{2,1,0:T(8,128)(2,1)} %copy.108) | copy-start | bytes 147460
  37.4 2.9 %copy-start.8 = (f32[96,2,4,128]{3,2,1,0:T(4,128)S(1)}, f32[96,2,4,128]{3,2,1,0:T(4,128)}, u32[]{:S(2)}) copy-start(f32[96,2,4,128]{3,2,1,0:T(4,128)} %get-tuple-element.38) | copy-start | bytes 1179652
  51.9 9.1 %copy-start.2 = (bf16[96,720]{1,0:T(8,128)(2,1)S(1)}, bf16[96,720]{1,0:T(8,128)(2,1)}, u32[]{:S(2)}) copy-start(bf16[96,720]{1,0:T(8,128)(2,1)} %x_ref.1) | copy-start | bytes 414724
  51.9 10.1 %copy-start.10 = (bf16[720,8]{0,1:T(8,128)(2,1)S(1)}, bf16[720,8]{0,1:T(8,128)(2,1)}, u32[]{:S(2)}) copy-start(bf16[720,8]{0,1:T(8,128)(2,1)} %param.22) | copy-start | bytes 34564
  61.2 38.8 %copy-start.4 = (f32[96,720]{1,0:T(8,128)}, f32[96,720]{1,0:T(8,128)S(1)}, u32[]{:S(2)}) copy-start(f32[96,720]{1,0:T(8,128)S(1)} %get-tuple-element.6) | copy-start | bytes 829444
  67.9 0.6 copy-start.3
  135.5 31.5 %all-to-all-start = ((bf16[8,1,48,720]{3,2,1,0:T(8,128)(2,1)}), bf16[8,1,48,720]{3,2,1,0:T(8,128)(2,1)}, u32[]{:S(2)}, u32[]{:S(2)}) async-start(bf16[8,1,48,720]{3,2,1,0:T(8,128)(2,1)} %bitcast.166), calls=%async_computation | async-start | bytes 1179648 | tf_op jit(solution)/shard_map/all_to_all | solution.py:479
  159.3 13.4 %copy-start.11 = (s32[96,4]{0,1:T(4,128)S(1)}, s32[96,4]{0,1:T(4,128)}, u32[]{:S(2)}) copy-start(s32[96,4]{0,1:T(4,128)} %param.25) | copy-start | bytes 4612
  164.8 8.1 %copy-start.5 = (f32[96,720]{1,0:T(8,128)S(1)}, f32[96,720]{1,0:T(8,128)}, u32[]{:S(2)}) copy-start(f32[96,720]{1,0:T(8,128)} %copy-done.4) | copy-start | bytes 829444
  167.0 22.4 %all-to-all-start.1 = ((bf16[8,1,48,720]{3,2,1,0:T(8,128)(2,1)}), bf16[8,1,48,720]{3,2,1,0:T(8,128)(2,1)}, u32[]{:S(2)}, u32[]{:S(2)}) async-start(bf16[8,1,48,720]{3,2,1,0:T(8,128)(2,1)} %bitcast.165), calls=%async_computation.1 | async-start | bytes 1179648 | tf_op jit(solution)/shard_map/all_to_all | solution.py:479
